TPU v7x, 32 devices: a whole 2x2x4 slice. The times are simulated.
32 devices in a mesh: scene: 2 (over x), along: 16 (over z, y, core).
Axes of the slice: x: 2, y: 2, z: 4, core: 2. Of those that a mesh axis runs over, the one named last changes fastest.
Arguments:
- echoes: bfloat16 [2, 64, 16, 16, 256], P(None, ('scene', 'along')), parts along dimension 1, may hold values from -6 to 6
- integer_cell_displacement: int32 [64, 16], P(('scene', 'along')), parts along dimension 0, may hold values from 0 to 15
- fractional_level_label: int32 [64, 16], P(('scene', 'along')), parts along dimension 0, may hold values from 0 to 15
- steering: bfloat16 [2, 256, 256], replicated, may hold values from -0.25 to 0.25
- tile_anchor: int32 [32], P('scene'), parts along dimension 0, may hold values from -64 to 3904, as said below
Outputs:
- image_tiles: bfloat16 [2, 8192, 256], P(None, ('scene', 'along')), parts along dimension 1
There are 2 independent parts, one for each index of `scene`. A program takes and returns all parts, laid end to end along the dimension named above; an argument that names none is the same for every part. Nothing has to cross between parts.
Inputs may be any that keep to these rules, and one draw needn't show every extreme that they name: tile_anchor[j] lies within 64 of j * 256.
All inputs are finite; a program needn't handle non-finite values.
Results may differ from a plain program's by a relative error of at most 0.0064.
Values may be sent and summed in bfloat16 or wider, within the bound.
No kernel may reach another device: no remote copies, remote signals or barrier semaphores. Data moves between devices by JAX's collectives and lax.ppermute only.
A program may use at most 64 MiB of HBM per device.

v0:
```python
import math

import jax
import jax.numpy as jnp
import numpy as np
from jax import lax
from jax.experimental import pallas as pl
from jax.experimental.pallas import tpu as pltpu
from jax.sharding import PartitionSpec as P


TILE_X = 256
STEPS = 16
TAPS = 8
SHIFTS = 16
FRACTION_LEVELS = 16
QUAD = 4093
WAVE_FOURTHS = 37
LANES = 128
FIRST_BLOCK = -2
UNITS = STEPS + 2
COARSE = 4
SPREAD = TAPS + COARSE - 1
F32 = jnp.float32
BF16 = jnp.bfloat16
VMEM = pl.BlockSpec(memory_space=pltpu.VMEM)
HBM = pl.BlockSpec(memory_space=pltpu.HBM)


def near(value):
    return pltpu.with_memory_space_constraint(value, pltpu.VMEM)


def far(value):
    return pltpu.with_memory_space_constraint(value, pltpu.HBM)


def filter_table():
    fraction = np.arange(FRACTION_LEVELS)[:, None] / FRACTION_LEVELS
    place = np.arange(TAPS)[None, :] - (TAPS // 2 - 1) - fraction
    return np.sinc(place) * (0.54 + 0.46 * np.cos(np.pi * place / (TAPS // 2)))


def circle_series():
    angle = np.cos(np.linspace(0, np.pi, 4001)) * np.pi
    odd = np.stack([angle ** (2 * k + 1) for k in range(6)], 1)
    even = np.stack([angle ** (2 * k) for k in range(7)], 1)
    sine = np.linalg.lstsq(odd, np.sin(angle), rcond=None)[0]
    cosine = np.linalg.lstsq(even, np.cos(angle), rcond=None)[0]
    return [float(c) for c in cosine], [float(c) for c in sine]


def horner(series, value):
    total = series[-1]
    for c in reversed(series[:-1]):
        total = total * value + c
    return total


def circle(turns, period, gain=1.0):
    cosine, sine = circle_series()
    angle = turns * (2.0 * math.pi / period)
    power = angle * angle
    return horner([c * gain for c in cosine], power), horner([c * gain for c in sine], power) * angle


def centred(value, period):
    return value - jnp.round(value * (1.0 / period)) * float(period)


def filter_pulses(cells, levels, echo, moved, store, core):
    _, pulses, tx, rx, bins = echo.shape
    chans = tx * rx
    half = bins // 2

    spread = lax.broadcasted_iota(jnp.int32, (tx, chans), 0) == lax.div(lax.broadcasted_iota(jnp.int32, (tx, chans), 1), rx)
    spread = spread.astype(F32)
    cell = jnp.dot(cells[...].astype(F32), spread, preferred_element_type=F32)
    level = jnp.dot(levels[...].astype(F32), spread, preferred_element_type=F32)
    coarse = jnp.floor(cell * (1.0 / COARSE))
    fine = cell - coarse * COARSE
    table = filter_table()
    weights = []
    for tap in range(TAPS):
        weight = jnp.zeros_like(level)
        for value in range(FRACTION_LEVELS):
            weight = jnp.where(level == float(value), float(table[value, tap]), weight)
        weights.append(weight)
    spread_weights = []
    for place in range(SPREAD):
        total = jnp.zeros_like(level)
        for step in range(COARSE):
            if 0 <= place - step < TAPS:
                total = jnp.where(fine == float(step), weights[place - step], total)
        spread_weights.append(total)
    period = 4 * FRACTION_LEVELS
    turn_cos, turn_sin = circle(centred(WAVE_FOURTHS * (cell * FRACTION_LEVELS + level), period), period)

    span = moved.shape[3]
    steps = SHIFTS // COARSE
    first = SHIFTS // 2 + TAPS // 2 - 1
    row = lax.broadcasted_iota(jnp.int32, (steps * span, bins), 0)
    shift = lax.div(row, span)
    wanted = half * core + row - span * shift - first + COARSE * shift
    select = (lax.broadcasted_iota(jnp.int32, (steps * span, bins), 1) == wanted).astype(F32).astype(BF16)

    for pulse in range(pulses):
        pick = coarse[pulse : pulse + 1]
        for part in range(2):
            rows = echo[part, pulse].reshape(chans, bins)
            shifted = lax.dot_general(select, rows, (((1,), (1,)), ((), ())), preferred_element_type=F32)
            value = shifted[:span]
            for step in range(1, steps):
                value = jnp.where(pick == float(step), shifted[step * span : (step + 1) * span], value)
            for lane in range(chans // LANES):
                moved[pulse, part, lane, :, :] = value[:, lane * LANES : (lane + 1) * LANES]
        for lane in range(chans // LANES):
            at = slice(lane * LANES, (lane + 1) * LANES)
            taps = [jnp.broadcast_to(w[pulse : pulse + 1, at], (8, LANES)) for w in spread_weights]
            lane_cos = jnp.broadcast_to(turn_cos[pulse : pulse + 1, at], (8, LANES))
            lane_sin = jnp.broadcast_to(turn_sin[pulse : pulse + 1, at], (8, LANES))
            for base in range(0, half, 16):
                reals, imags = [], []
                for begin in (base, base + 8):
                    sums = []
                    for part in range(2):
                        total = taps[0] * moved[pulse, part, lane, begin : begin + 8, :]
                        for tap in range(1, SPREAD):
                            total = total + taps[tap] * moved[pulse, part, lane, begin + tap : begin + tap + 8, :]
                        sums.append(total)
                    reals.append(sums[0] * lane_cos + sums[1] * lane_sin)
                    imags.append(sums[1] * lane_cos - sums[0] * lane_sin)
                store(pulse, slice(base, base + 16), at, jnp.concatenate(reals, 0).astype(BF16))
                at_imag = slice(chans + lane * LANES, chans + (lane + 1) * LANES)
                store(pulse, slice(base, base + 16), at_imag, jnp.concatenate(imags, 0).astype(BF16))


def first_kernel(cells, levels, echo, steering, turned, mixer, near_cells, near_levels, near_echo, near_steering, moved, sems):
    copies = [
        pltpu.make_async_copy(source, target, sems.at[index])
        for index, (source, target) in enumerate(
            ((cells, near_cells), (levels, near_levels), (echo, near_echo), (steering, near_steering))
        )
    ]
    for copy in copies:
        copy.start()
    for copy in copies[:3]:
        copy.wait()

    def store(pulse, rows, lanes, value):
        turned[pulse, rows, lanes] = value

    filter_pulses(near_cells, near_levels, near_echo, moved, store, lax.rem(lax.axis_index("along"), 2))
    copies[3].wait()
    _, chans, beams = steering.shape
    real, imag = near_steering[0], near_steering[1]
    mixer[:chans, :beams] = real
    mixer[:chans, beams:] = imag
    mixer[chans:, :beams] = -imag
    mixer[chans:, beams:] = real


def second_kernel(cells, levels, echo, own, *rest, chips):
    outs, (moved, turned) = rest[:-2], rest[-2:]
    pulses = echo.shape[1]
    half = own.shape[1]
    me = lax.axis_index("along")
    core = lax.rem(me, 2)
    chip = lax.div(me, 2)

    def store(pulse, rows, lanes, value):
        turned[pulse, rows, lanes] = value

    filter_pulses(cells, levels, echo, moved, store, core)
    own_place = core * pulses
    other_place = (1 - core) * pulses
    if len(outs) == 1:
        outs[0][pl.ds(own_place, pulses)] = own[...]
        outs[0][pl.ds(other_place, pulses)] = turned[...]
    else:
        width = half // chips
        for step, out in enumerate(outs):
            begin = pl.multiple_of(jnp.bitwise_xor(chip, step) * width, width)
            out[pl.ds(own_place, pulses)] = own[:, pl.ds(begin, width), :]
            out[pl.ds(other_place, pulses)] = turned[:, pl.ds(begin, width), :]


def filter_first(cells, levels, echoes, steering):
    _, pulses, _, _, bins = echoes.shape
    _, chans, beams = steering.shape
    return pl.pallas_call(
        first_kernel,
        out_shape=(pltpu.VMEM((pulses, bins // 2, 2 * chans), BF16), pltpu.VMEM((2 * chans, 2 * beams), BF16)),
        in_specs=[HBM] * 4,
        out_specs=(VMEM, VMEM),
        scratch_shapes=[
            pltpu.VMEM(cells.shape, jnp.int32),
            pltpu.VMEM(levels.shape, jnp.int32),
            pltpu.VMEM(echoes.shape, BF16),
            pltpu.VMEM(steering.shape, BF16),
            pltpu.VMEM((pulses, 2, chans // LANES, bins // 2 + 16, LANES), F32),
            pltpu.SemaphoreType.DMA((4,)),
        ],
        compiler_params=pltpu.CompilerParams(vmem_limit_bytes=16 << 20),
        cost_estimate=pl.CostEstimate(flops=10**8, transcendentals=0, bytes_accessed=0),
        name="filter_first",
    )(far(cells), far(levels), far(echoes), far(steering))


def filter_second(cells, levels, echoes, own, chips):
    _, pulses, tx, rx, bins = echoes.shape
    half, chans = bins // 2, tx * rx
    width = half // chips
    direct = width % 16 == 0
    count = chips if direct else 1

    def kernel(*refs):
        second_kernel(*refs, chips=chips)

    shape = (2 * pulses, width if direct else half, 2 * chans)
    done = pl.pallas_call(
        kernel,
        out_shape=[pltpu.VMEM(shape, BF16)] * count,
        in_specs=[VMEM] * 4,
        out_specs=[VMEM] * count,
        scratch_shapes=[
            pltpu.VMEM((pulses, 2, chans // LANES, half + 16, LANES), F32),
            pltpu.VMEM((pulses, half, 2 * chans), BF16),
        ],
        compiler_params=pltpu.CompilerParams(vmem_limit_bytes=16 << 20),
        name="filter_second",
    )(near(cells), near(levels), near(echoes), near(own))
    if direct:
        return done
    chip = lax.axis_index("along") // 2
    split = done[0].reshape(2 * pulses, chips, width, 2 * chans)
    return [lax.dynamic_index_in_dim(split, jnp.bitwise_xor(chip, k), 1, False) for k in range(chips)]


def table_kernel(table, *, beams, gain):
    step = 32
    lane = lax.broadcasted_iota(jnp.int32, (step, LANES), 1).astype(F32) + float(FIRST_BLOCK * LANES)
    offset = centred(lane, QUAD)
    square = centred(offset * offset, QUAD)
    ahead = centred(2.0 * LANES * offset + LANES * LANES, QUAD)
    for row in range(0, beams, step):
        beam = (lax.broadcasted_iota(jnp.int32, (step, LANES), 0) + row).astype(F32)
        beam_square = centred(beam * beam, QUAD)
        beam_next = beam + 1.0
        state = circle(centred(beam_next * square + beam_square * offset, QUAD), QUAD, gain)
        growth = circle(centred(beam_next * ahead + float(LANES) * beam_square, QUAD), QUAD)
        bend_cos, bend_sin = circle(centred(beam_next * float(2 * LANES * LANES % QUAD), QUAD), QUAD)

        def block(index, carry, row=row, bend_cos=bend_cos, bend_sin=bend_sin):
            state_cos, state_sin, growth_cos, growth_sin = carry
            at = pl.ds(pl.multiple_of(index * LANES, LANES), LANES)
            table[row : row + step, at] = state_cos.astype(BF16)
            table[beams + row : beams + row + step, at] = state_sin.astype(BF16)
            return (
                state_cos * growth_cos - state_sin * growth_sin,
                state_cos * growth_sin + state_sin * growth_cos,
                growth_cos * bend_cos - growth_sin * bend_sin,
                growth_cos * bend_sin + growth_sin * bend_cos,
            )

        lax.fori_loop(0, 2 * UNITS, block, (*state, *growth), unroll=4)


def make_table(beams, pulses):
    gain = (STEPS * pulses * beams) ** -0.5

    def kernel(*refs):
        table_kernel(*refs, beams=beams, gain=gain)

    return pl.pallas_call(
        kernel,
        out_shape=pltpu.VMEM((2 * beams, 2 * UNITS * LANES), BF16),
        in_specs=[],
        out_specs=VMEM,
        compiler_params=pltpu.CompilerParams(vmem_limit_bytes=16 << 20),
        cost_estimate=pl.CostEstimate(flops=40 * beams * 2 * UNITS * LANES * 100, transcendentals=0, bytes_accessed=0),
        name="table",
    )()


def project_kernel(anchors, mixer, table, *rest, pulses, tiles, width, beams):
    pieces, (out, data, left, right, common, edge_first, edge_low, edge_high, edge_last) = rest[:-9], rest[-9:]
    rows = pulses * width
    if len(pieces) == 1:
        gathered = pieces[0][...]
    else:
        chip = lax.div(lax.axis_index("along"), 2)
        part = rows // len(pieces)
        for step, piece in enumerate(pieces):
            begin = pl.multiple_of(jnp.bitwise_xor(chip, step) * part, part)
            data[pl.ds(begin, part), :] = piece[...].reshape(part, data.shape[1])
        gathered = data[...]
    formed = jnp.dot(gathered, mixer[...], preferred_element_type=F32)
    real = formed[:, :beams].astype(BF16)
    imag = formed[:, beams:].astype(BF16)
    left[:, :beams] = real
    left[:, beams:] = -imag
    right[:, :beams] = imag
    right[:, beams:] = real
    last_block = 2 * tiles

    def used(first):
        count = min(pulses, last_block - first + 1)
        return min(rows, -(-count * width // 16) * 16)

    def product(first, count):
        unit = (first - FIRST_BLOCK) // 2
        part = table[:, unit * 2 * LANES : (unit + 1) * 2 * LANES]
        return [jnp.dot(side[:count, :], part, preferred_element_type=F32) for side in (left, right)]

    for c, value in enumerate(product(0, rows)):
        edge_low[c, :rows, :] = value[:, :LANES]
        common[c, :rows, :LANES] = jnp.zeros((rows, LANES), F32)
        common[c, :rows, LANES:] = value[:, LANES:]
        common[c, rows:, :] = jnp.zeros((common.shape[1] - rows, 2 * LANES), F32)
    for c, value in enumerate(product(FIRST_BLOCK, rows)):
        edge_first[c] = value
    for first in range(2, 2 * STEPS - 2, 2):
        if first > last_block:
            break
        count = used(first)
        for c, value in enumerate(product(first, count)):
            at = slice(first * width, first * width + count)
            common[c, at, :] = common[c, at, :] + value
    for first, edge in ((2 * STEPS - 2, edge_high), (2 * STEPS, edge_last)):
        if first <= last_block:
            count = used(first)
            for c, value in enumerate(product(first, count)):
                edge[c, :count, :] = value

    lane = lax.broadcasted_iota(jnp.int32, (1, LANES), 1)

    def take(source, c, block, first, half):
        pulse = block - first
        if first > last_block or not 0 <= pulse < pulses:
            return []
        lanes = slice(half * LANES, (half + 1) * LANES)
        return [source[c, pulse * width : (pulse + 1) * width, lanes]]

    def total(parts):
        value = parts[0]
        for part in parts[1:]:
            value = value + part
        return value

    for tile in range(tiles):
        start = anchors[tile] - tile * TILE_X + LANES
        far = start >= LANES
        amount = jnp.bitwise_and(-start, LANES - 1)
        keep = lane < LANES - jnp.bitwise_and(start, LANES - 1)
        for c in range(2):
            blocks = []
            for kind in (-1, 0, 1, 2):
                block = 2 * tile + kind
                parts = []
                if 0 <= block:
                    parts += [common[c, block * width : (block + 1) * width, :LANES]]
                if kind == -1:
                    parts += take(edge_first, c, block, FIRST_BLOCK, 0)
                if kind < 2:
                    parts += take(edge_low, c, block, 0, 0)
                if kind > -1:
                    parts += take(edge_high, c, block, 2 * STEPS - 2, 0)
                if kind == 2:
                    parts += take(edge_last, c, block, 2 * STEPS, 0)
                if 0 <= block - 1:
                    parts += [common[c, (block - 1) * width : block * width, LANES:]]
                if kind < 1:
                    parts += take(edge_first, c, block - 1, FIRST_BLOCK, 1)
                else:
                    parts += take(edge_high, c, block - 1, 2 * STEPS - 2, 1)
                blocks.append(total(parts))
            close = [jnp.where(far, blocks[k + 1], blocks[k]) for k in range(3)]
            moved = [pltpu.roll(value, amount, 1) for value in close]
            for half in range(2):
                value = jnp.where(keep, moved[half], moved[half + 1])
                out[tile, c, :, half * LANES : (half + 1) * LANES] = value.astype(BF16)


def project(anchors, pieces, mixer, table, pulses, width):
    rows = pulses * width
    tiles = anchors.shape[0]
    chans, beams = mixer.shape[0], mixer.shape[1] // 2
    span = -(-(2 * tiles + 2) * width // 16) * 16 + 16

    def kernel(*refs):
        project_kernel(*refs, pulses=pulses, tiles=tiles, width=width, beams=beams)

    return pl.pallas_call(
        kernel,
        out_shape=pltpu.VMEM((tiles, 2, width, TILE_X), BF16),
        in_specs=[pl.BlockSpec(memory_space=pltpu.SMEM)] + [VMEM] * (2 + len(pieces)),
        out_specs=VMEM,
        scratch_shapes=[
            pltpu.VMEM((rows, chans), BF16),
            pltpu.VMEM((rows, 2 * beams), BF16),
            pltpu.VMEM((rows, 2 * beams), BF16),
            pltpu.VMEM((2, span, 2 * LANES), F32),
            pltpu.VMEM((2, rows, 2 * LANES), F32),
            pltpu.VMEM((2, rows, LANES), F32),
            pltpu.VMEM((2, rows, 2 * LANES), F32),
            pltpu.VMEM((2, rows, 2 * LANES), F32),
        ],
        compiler_params=pltpu.CompilerParams(vmem_limit_bytes=24 << 20),
        name="project",
    )(anchors, near(mixer), near(table), *[near(piece) for piece in pieces])


def turn_kernel(data, out):
    count, _, _, pixels = data.shape
    order = [chip * 2 + core for core in range(2) for chip in range(count // 2)]
    same = lax.broadcasted_iota(jnp.int32, (pixels, pixels), 0) == lax.broadcasted_iota(jnp.int32, (pixels, pixels), 1)
    same = same.astype(F32).astype(BF16)
    for c in range(2):
        value = jnp.concatenate([data[source, c] for source in order], 0)
        out[c] = lax.dot_general(same, value, (((1,), (1,)), ((), ())), preferred_element_type=F32).astype(BF16)


def turn(data):
    count, _, width, pixels = data.shape
    if width % 16:
        data = data.reshape(count // 2, 2, 2, width, pixels)
        return data.transpose(2, 4, 1, 0, 3).reshape(2, pixels, count * width)
    return pl.pallas_call(
        turn_kernel,
        out_shape=jax.ShapeDtypeStruct((2, pixels, count * width), BF16),
        in_specs=[VMEM],
        out_specs=VMEM,
        compiler_params=pltpu.CompilerParams(vmem_limit_bytes=16 << 20),
        name="turn",
    )(near(data))


def far_first(chips):
    order = []
    for bit in reversed(range((chips - 1).bit_length())):
        order += [k for k in range(1 << bit, min(2 << bit, chips))]
    return order


def local(echoes, integer_cell_displacement, fractional_level_label, steering, tile_anchor):
    devices = lax.axis_size("along")
    chips = devices // 2
    pulses, bins = echoes.shape[1], echoes.shape[4]
    width = bins // devices

    def from_pair(value, step):
        return lax.ppermute(value, "along", [(i, i ^ step) for i in range(devices)])

    other_cells, other_levels, other = [
        from_pair(value, 1) for value in (integer_cell_displacement, fractional_level_label, echoes)
    ]
    own, mixer = filter_first(integer_cell_displacement, fractional_level_label, echoes, steering)
    sent = filter_second(other_cells, other_levels, other, own, chips)
    table = make_table(steering.shape[2], pulses)
    pieces = [sent[0]] + [None] * (chips - 1)
    for k in far_first(chips):
        pieces[k] = from_pair(sent[k], 2 * k)
    if width % 16:
        chip = lax.axis_index("along") // 2
        order = jnp.bitwise_xor(jnp.arange(chips), chip)
        pieces = [jnp.take(jnp.stack(pieces), order, axis=0).reshape(devices * pulses * width, -1)]
    finished = project(tile_anchor, pieces, mixer, table, devices * pulses, width)
    return turn(lax.all_to_all(finished, "along", 0, 0, tiled=True))


def solution(mesh):
    placed = (
        P(None, ("scene", "along"), None, None, None),
        P(("scene", "along"), None),
        P(("scene", "along"), None),
        P(),
        P("scene"),
    )
    return jax.shard_map(
        local,
        mesh=mesh,
        in_specs=placed,
        out_specs=P(None, ("scene", "along"), None),
        check_vma=False,
    )
```

profile of v0, /device:TPU:0, one launch (start us, length us, event | category | flops | bytes accessed | tf_op | source)
XLA Modules:
  0.0 42.8 jit_solution(8900962821159006492)
XLA Ops:
  0.0 0.5 %collective-permute-start.2 = (bf16[2,2,16,16,256]{4,3,2,1,0:T(8,128)(2,1)}, bf16[2,2,16,16,256]{4,3,2,1,0:T(8,128)(2,1)S(1)}, u32[]{:S(2)}, u32[]{:S(2)}) collective-permute-start(bf16[2,2,16,16,256]{4,3,2,1,0:T(8,128)(2,1)} %echo.1), channel_id=1, source_target_pairs={{0,1},{1,0},{2,3},{3,2},{4,5},{5,4},{6,7},{7,6},{8,9},{9,8},{10,11... | collective-permute-start | bytes 1572872 | tf_op jit(solution)/shard_map/ppermute | solution.py:453
  0.5 0.0 collective-permute-start
  0.5 0.5 %collective-permute-start.1 = (s32[2,16]{1,0:T(2,128)}, s32[2,16]{1,0:T(2,128)S(1)}, u32[]{:S(2)}, u32[]{:S(2)}) collective-permute-start(s32[2,16]{1,0:T(2,128)} %levels.1), channel_id=1, source_target_pairs={{0,1},{1,0},{2,3},{3,2},{4,5},{5,4},{6,7},{7,6},{8,9},{9,8},{10,11... | collective-permute-start | bytes 392 | tf_op jit(solution)/shard_map/ppermute | solution.py:453
  1.0 2.2 %filter_first.1 = (bf16[2,128,512]{2,1,0:T(8,128)(2,1)S(1)}, bf16[512,512]{1,0:T(8,128)(2,1)S(1)}) custom-call(s32[2,16]{1,0:T(2,128)} %cells.1, s32[2,16]{1,0:T(2,128)} %levels.1, bf16[2,2,16,16,256]{4,3,2,1,0:T(8,128)(2,1)} %echo.1, bf16[2,256,256]{2,1,0:T(8,128)(2,1)} %steering.1), custom_call_target="tpu_custom_call" | custom-call | flops 100000000 | tf_op jit(solution)/shard_map/filter_first/pallas_call | solution.py:191
  3.2 0.0 collective-permute-done.refs_0_
  3.2 0.0 collective-permute-done.1.refs_1_
  3.2 0.0 collective-permute-done.2.refs_2_
  3.2 1.0 %filter_second.1 = (bf16[4,16,512]{2,1,0:T(8,128)(2,1)S(1)}, bf16[4,16,512]{2,1,0:T(8,128)(2,1)S(1)}, bf16[4,16,512]{2,1,0:T(8,128)(2,1)S(1)}, bf16[4,16,512]{2,...) custom-call(s32[2,16]{1,0:T(2,128)S(1)} %collective-permute-done.ref, ...), custom_call_target="tpu_custom_call" | custom-call | tf_op jit(solution)/shard_map/filter_second/pallas_call | solution.py:221
  4.2 2.6 %collective-permute-start.3 = (bf16[4,16,512]{2,1,0:T(8,128)(2,1)S(1)}, bf16[4,16,512]{2,1,0:T(8,128)(2,1)S(1)}, u32[]{:S(2)}, u32[]{:S(2)}) collective-permute-start(bf16[4,16,512]{2,1,0:T(8,128)(2,1)S(1)} %get-tuple-element.18), channel_id=1, source_target_pairs={{0,2},{1,3},{2,0},{3,1},{4,6},{5,7},{6,4},{7,5},{8,10},{9,11},{10,... | collective-permute-start | bytes 196616 | tf_op jit(solution)/shard_map/ppermute | solution.py:453
  6.8 1.6 %collective-permute-start.4 = (bf16[4,16,512]{2,1,0:T(8,128)(2,1)S(1)}, bf16[4,16,512]{2,1,0:T(8,128)(2,1)S(1)}, u32[]{:S(2)}, u32[]{:S(2)}) collective-permute-start(bf16[4,16,512]{2,1,0:T(8,128)(2,1)S(1)} %get-tuple-element.19), channel_id=1, source_target_pairs={{0,4},{1,5},{2,6},{3,7},{4,0},{5,1},{6,2},{7,3},{8,12},{9,13},{10,... | collective-permute-start | bytes 196616 | tf_op jit(solution)/shard_map/ppermute | solution.py:453
  8.4 0.0 collective-permute-start.5
  8.4 3.0 %collective-permute-start.6 = (bf16[4,16,512]{2,1,0:T(8,128)(2,1)S(1)}, bf16[4,16,512]{2,1,0:T(8,128)(2,1)S(1)}, u32[]{:S(2)}, u32[]{:S(2)}) collective-permute-start(bf16[4,16,512]{2,1,0:T(8,128)(2,1)S(1)} %get-tuple-element.21), channel_id=1, source_target_pairs={{0,8},{1,9},{2,10},{3,11},{4,12},{5,13},{6,14},{7,15},{8,0},{9,1},... | collective-permute-start | bytes 196616 | tf_op jit(solution)/shard_map/ppermute | solution.py:453
  11.4 1.3 %collective-permute-start.7 = (bf16[4,16,512]{2,1,0:T(8,128)(2,1)S(1)}, bf16[4,16,512]{2,1,0:T(8,128)(2,1)S(1)}, u32[]{:S(2)}, u32[]{:S(2)}) collective-permute-start(bf16[4,16,512]{2,1,0:T(8,128)(2,1)S(1)} %get-tuple-element.22), channel_id=1, source_target_pairs={{0,10},{1,11},{2,8},{3,9},{4,14},{5,15},{6,12},{7,13},{8,2},{9,3},... | collective-permute-start | bytes 196616 | tf_op jit(solution)/shard_map/ppermute | solution.py:453
  12.7 0.0 collective-permute-done.3.refs_4_
  12.7 3.6 %collective-permute-start.8 = (bf16[4,16,512]{2,1,0:T(8,128)(2,1)S(1)}, bf16[4,16,512]{2,1,0:T(8,128)(2,1)S(1)}, u32[]{:S(2)}, u32[]{:S(2)}) collective-permute-start(bf16[4,16,512]{2,1,0:T(8,128)(2,1)S(1)} %get-tuple-element.23), channel_id=1, source_target_pairs={{0,12},{1,13},{2,14},{3,15},{4,8},{5,9},{6,10},{7,11},{8,4},{9,5},... | collective-permute-start | bytes 196616 | tf_op jit(solution)/shard_map/ppermute | solution.py:453
  16.3 0.0 collective-permute-done.4.refs_5_
  16.3 0.0 copy-start
  16.3 0.0 collective-permute-start.9
  16.3 3.0 %table.1.refs_2_ = bf16[512,4608]{1,0:T(8,128)(2,1)S(1)} custom-call(), custom_call_target="tpu_custom_call" | custom-call | flops 4718592000 | tf_op jit(solution)/shard_map/table/pallas_call | solution.py:275
  19.3 0.0 collective-permute-done.5.refs_6_
  19.3 0.0 collective-permute-done.6.refs_7_
  19.3 2.3 %collective-permute-done.7.refs_8_ = bf16[4,16,512]{2,1,0:T(8,128)(2,1)S(1)} collective-permute-done((bf16[4,16,512]{2,1,0:T(8,128)(2,1)S(1)}, bf16[4,16,512]{2,1,0:T(8,128)(2,1)S(1)}, u32[]{:S(2)}, u32[]{:S(2)}) %collective-permute-start.7) | collective-permute-done | bytes 65568 | tf_op jit(solution)/shard_map/ppermute | solution.py:453
  21.6 0.0 collective-permute-done.8.refs_9_
  21.6 1.8 %collective-permute-done.9.refs_10_ = bf16[4,16,512]{2,1,0:T(8,128)(2,1)S(1)} collective-permute-done((bf16[4,16,512]{2,1,0:T(8,128)(2,1)S(1)}, bf16[4,16,512]{2,1,0:T(8,128)(2,1)S(1)}, u32[]{:S(2)}, u32[]{:S(2)}) %collective-permute-start.9) | collective-permute-done | bytes 65568 | tf_op jit(solution)/shard_map/ppermute | solution.py:453
  23.4 0.0 copy-done
  23.4 3.9 %project.1 = bf16[16,2,16,256]{3,2,1,0:T(8,128)(2,1)S(1)} custom-call(s32[16]{0:T(128)S(1)} %copy-done, bf16[512,512]{1,0:T(8,128)(2,1)S(1)} %get-tuple-element.15.refs_1_, bf16[512,4608]{1,0:T(8,128)(2,1)S(1)} %table.1.refs_2_, bf16[4,16,512]{2,1,0:T(8,128)(2,1)S(1)} %get-tuple-element.17.refs_3_, bf16[4,16,512]{2,1,0:T(8,128)(2,1)S(1)} %collective-permute-done.3.refs_4_, ...), custom_call_target="tpu_custom_call" | custom-call | tf_op jit(solution)/shard_map/project/pallas_call | solution.py:394
  27.3 14.6 %all_to_all.5.data = bf16[16,2,16,256]{3,2,1,0:T(8,128)(2,1)S(1)} all-to-all(bf16[16,2,16,256]{3,2,1,0:T(8,128)(2,1)S(1)} %project.1), channel_id=1, replica_groups=mesh['scene'=2,'along'=16] {'along'}, dimensions={0} | all-to-all | bytes 524288 | tf_op jit(solution)/shard_map/all_to_all | solution.py:469
  41.9 1.0 %turn.1 = bf16[2,256,256]{2,1,0:T(8,128)(2,1)} custom-call(bf16[16,2,16,256]{3,2,1,0:T(8,128)(2,1)S(1)} %all_to_all.5.data), custom_call_target="tpu_custom_call" | custom-call | tf_op jit(solution)/shard_map/turn/pallas_call | solution.py:429
Async XLA Ops:
  0.0 3.2 %collective-permute-start.2 = (bf16[2,2,16,16,256]{4,3,2,1,0:T(8,128)(2,1)}, bf16[2,2,16,16,256]{4,3,2,1,0:T(8,128)(2,1)S(1)}, u32[]{:S(2)}, u32[]{:S(2)}) collective-permute-start(bf16[2,2,16,16,256]{4,3,2,1,0:T(8,128)(2,1)} %echo.1), channel_id=1, source_target_pairs={{0,1},{1,0},{2,3},{3,2},{4,5},{5,4},{6,7},{7,6},{8,9},{9,8},{10,11... | collective-permute-start | bytes 1572872 | tf_op jit(solution)/shard_map/ppermute | solution.py:453
  0.5 2.7 %collective-permute-start = (s32[2,16]{1,0:T(2,128)}, s32[2,16]{1,0:T(2,128)S(1)}, u32[]{:S(2)}, u32[]{:S(2)}) collective-permute-start(s32[2,16]{1,0:T(2,128)} %cells.1), channel_id=1, source_target_pairs={{0,1},{1,0},{2,3},{3,2},{4,5},{5,4},{6,7},{7,6},{8,9},{9,8},{10,11... | collective-permute-start | bytes 392 | tf_op jit(solution)/shard_map/ppermute | solution.py:453
  0.5 2.7 %collective-permute-start.1 = (s32[2,16]{1,0:T(2,128)}, s32[2,16]{1,0:T(2,128)S(1)}, u32[]{:S(2)}, u32[]{:S(2)}) collective-permute-start(s32[2,16]{1,0:T(2,128)} %levels.1), channel_id=1, source_target_pairs={{0,1},{1,0},{2,3},{3,2},{4,5},{5,4},{6,7},{7,6},{8,9},{9,8},{10,11... | collective-permute-start | bytes 392 | tf_op jit(solution)/shard_map/ppermute | solution.py:453
  4.2 8.4 %collective-permute-start.3 = (bf16[4,16,512]{2,1,0:T(8,128)(2,1)S(1)}, bf16[4,16,512]{2,1,0:T(8,128)(2,1)S(1)}, u32[]{:S(2)}, u32[]{:S(2)}) collective-permute-start(bf16[4,16,512]{2,1,0:T(8,128)(2,1)S(1)} %get-tuple-element.18), channel_id=1, source_target_pairs={{0,2},{1,3},{2,0},{3,1},{4,6},{5,7},{6,4},{7,5},{8,10},{9,11},{10,... | collective-permute-start | bytes 196616 | tf_op jit(solution)/shard_map/ppermute | solution.py:453
  6.8 9.5 %collective-permute-start.4 = (bf16[4,16,512]{2,1,0:T(8,128)(2,1)S(1)}, bf16[4,16,512]{2,1,0:T(8,128)(2,1)S(1)}, u32[]{:S(2)}, u32[]{:S(2)}) collective-permute-start(bf16[4,16,512]{2,1,0:T(8,128)(2,1)S(1)} %get-tuple-element.19), channel_id=1, source_target_pairs={{0,4},{1,5},{2,6},{3,7},{4,0},{5,1},{6,2},{7,3},{8,12},{9,13},{10,... | collective-permute-start | bytes 196616 | tf_op jit(solution)/shard_map/ppermute | solution.py:453
  8.4 10.9 %collective-permute-start.5 = (bf16[4,16,512]{2,1,0:T(8,128)(2,1)S(1)}, bf16[4,16,512]{2,1,0:T(8,128)(2,1)S(1)}, u32[]{:S(2)}, u32[]{:S(2)}) collective-permute-start(bf16[4,16,512]{2,1,0:T(8,128)(2,1)S(1)} %get-tuple-element.20), channel_id=1, source_target_pairs={{0,6},{1,7},{2,4},{3,5},{4,2},{5,3},{6,0},{7,1},{8,14},{9,15},{10,... | collective-permute-start | bytes 196616 | tf_op jit(solution)/shard_map/ppermute | solution.py:453
  8.4 10.9 %collective-permute-start.6 = (bf16[4,16,512]{2,1,0:T(8,128)(2,1)S(1)}, bf16[4,16,512]{2,1,0:T(8,128)(2,1)S(1)}, u32[]{:S(2)}, u32[]{:S(2)}) collective-permute-start(bf16[4,16,512]{2,1,0:T(8,128)(2,1)S(1)} %get-tuple-element.21), channel_id=1, source_target_pairs={{0,8},{1,9},{2,10},{3,11},{4,12},{5,13},{6,14},{7,15},{8,0},{9,1},... | collective-permute-start | bytes 196616 | tf_op jit(solution)/shard_map/ppermute | solution.py:453
  11.4 10.2 %collective-permute-start.7 = (bf16[4,16,512]{2,1,0:T(8,128)(2,1)S(1)}, bf16[4,16,512]{2,1,0:T(8,128)(2,1)S(1)}, u32[]{:S(2)}, u32[]{:S(2)}) collective-permute-start(bf16[4,16,512]{2,1,0:T(8,128)(2,1)S(1)} %get-tuple-element.22), channel_id=1, source_target_pairs={{0,10},{1,11},{2,8},{3,9},{4,14},{5,15},{6,12},{7,13},{8,2},{9,3},... | collective-permute-start | bytes 196616 | tf_op jit(solution)/shard_map/ppermute | solution.py:453
  12.7 8.9 %collective-permute-start.8 = (bf16[4,16,512]{2,1,0:T(8,128)(2,1)S(1)}, bf16[4,16,512]{2,1,0:T(8,128)(2,1)S(1)}, u32[]{:S(2)}, u32[]{:S(2)}) collective-permute-start(bf16[4,16,512]{2,1,0:T(8,128)(2,1)S(1)} %get-tuple-element.23), channel_id=1, source_target_pairs={{0,12},{1,13},{2,14},{3,15},{4,8},{5,9},{6,10},{7,11},{8,4},{9,5},... | collective-permute-start | bytes 196616 | tf_op jit(solution)/shard_map/ppermute | solution.py:453
  16.3 7.1 %copy-start = (s32[16]{0:T(128)S(1)}, s32[16]{0:T(128)}, u32[]{:S(2)}) copy-start(s32[16]{0:T(128)} %refs_0_.1) | copy-start | bytes 196
  16.3 7.1 %collective-permute-start.9 = (bf16[4,16,512]{2,1,0:T(8,128)(2,1)S(1)}, bf16[4,16,512]{2,1,0:T(8,128)(2,1)S(1)}, u32[]{:S(2)}, u32[]{:S(2)}) collective-permute-start(bf16[4,16,512]{2,1,0:T(8,128)(2,1)S(1)} %get-tuple-element.24), channel_id=1, source_target_pairs={{0,14},{1,15},{2,12},{3,13},{4,10},{5,11},{6,8},{7,9},{8,6},{9,7},... | collective-permute-start | bytes 196616 | tf_op jit(solution)/shard_map/ppermute | solution.py:453
where the time goes:
time: 43 us; the launch traced here: 42.8 us
  blocking collectives  14.6 us (34%)
  starting transfers between devices  13.1 us (30%)
  Pallas kernels  11.1 us (26%)
  waiting for transfers between devices  4.06 us (9%)
    all_to_all x1, blocking collectives, local(): return turn(lax.all_to_all(finished, 'along', 0, 0, tiled=True))  14.6 us
    ppermute x10, starting transfers between devices, from_pair(): return lax.ppermute(value, 'along', [(i, i ^ step) for i in range(devices)])  13.1 us
    ppermute x10, waiting for transfers between devices, from_pair(): return lax.ppermute(value, 'along', [(i, i ^ step) for i in range(devices)])  4.06 us
    pallas_call x1, Pallas kernels, project(): pl.pallas_call(kernel, out_shape=pltpu.VMEM((tiles, 2, width, TILE_X), BF...  3.94 us
    pallas_call x1, Pallas kernels, make_table(): pl.pallas_call(kernel, out_shape=pltpu.VMEM((2 * beams, 2 * UNITS * LANES...  2.97 us
    pallas_call x1, Pallas kernels, filter_first(): pl.pallas_call(first_kernel, out_shape=(pltpu.VMEM((pulses, bins // 2, 2...  2.16 us
    pallas_call x1, Pallas kernels, filter_second(): pl.pallas_call(kernel, out_shape=[pltpu.VMEM(shape, BF16)] * count, in_sp...  1.04 us
    pallas_call x1, Pallas kernels, turn(): pl.pallas_call(turn_kernel, out_shape=jax.ShapeDtypeStruct((2, pixels, co...  0.97 us
  transfers between devices with their start and end apart: 10, of which 2 were waited for; matrix products, arithmetic and copies ran while one was open for 0% of the time, Pallas kernels for 12%

commit v1 on v0

--- a/solution.py
+++ b/solution.py
@@ -160,13 +160,13 @@
     mixer[chans:, beams:] = real
 
 
-def second_kernel(cells, levels, echo, own, *rest, chips):
+def second_kernel(cells, levels, echo, own, *rest, group):
     outs, (moved, turned) = rest[:-2], rest[-2:]
     pulses = echo.shape[1]
     half = own.shape[1]
     me = lax.axis_index("along")
     core = lax.rem(me, 2)
-    chip = lax.div(me, 2)
+    chip = lax.rem(lax.div(me, 2), group)
 
     def store(pulse, rows, lanes, value):
         turned[pulse, rows, lanes] = value
@@ -178,7 +178,7 @@
         outs[0][pl.ds(own_place, pulses)] = own[...]
         outs[0][pl.ds(other_place, pulses)] = turned[...]
     else:
-        width = half // chips
+        width = half // group
         for step, out in enumerate(outs):
             begin = pl.multiple_of(jnp.bitwise_xor(chip, step) * width, width)
             out[pl.ds(own_place, pulses)] = own[:, pl.ds(begin, width), :]
@@ -207,15 +207,15 @@
     )(far(cells), far(levels), far(echoes), far(steering))
 
 
-def filter_second(cells, levels, echoes, own, chips):
+def filter_second(cells, levels, echoes, own, group):
     _, pulses, tx, rx, bins = echoes.shape
     half, chans = bins // 2, tx * rx
-    width = half // chips
+    width = half // group
     direct = width % 16 == 0
-    count = chips if direct else 1
+    count = group if direct else 1
 
     def kernel(*refs):
-        second_kernel(*refs, chips=chips)
+        second_kernel(*refs, group=group)
 
     shape = (2 * pulses, width if direct else half, 2 * chans)
     done = pl.pallas_call(
@@ -232,9 +232,9 @@
     )(near(cells), near(levels), near(echoes), near(own))
     if direct:
         return done
-    chip = lax.axis_index("along") // 2
-    split = done[0].reshape(2 * pulses, chips, width, 2 * chans)
-    return [lax.dynamic_index_in_dim(split, jnp.bitwise_xor(chip, k), 1, False) for k in range(chips)]
+    chip = lax.axis_index("along") // 2 % group
+    split = done[0].reshape(2 * pulses, group, width, 2 * chans)
+    return [lax.dynamic_index_in_dim(split, jnp.bitwise_xor(chip, k), 1, False) for k in range(group)]
 
 
 def table_kernel(table, *, beams, gain):
@@ -283,25 +283,49 @@
     )()
 
 
-def project_kernel(anchors, mixer, table, *rest, pulses, tiles, width, beams):
-    pieces, (out, data, left, right, common, edge_first, edge_low, edge_high, edge_last) = rest[:-9], rest[-9:]
-    rows = pulses * width
-    if len(pieces) == 1:
-        gathered = pieces[0][...]
-    else:
-        chip = lax.div(lax.axis_index("along"), 2)
-        part = rows // len(pieces)
-        for step, piece in enumerate(pieces):
-            begin = pl.multiple_of(jnp.bitwise_xor(chip, step) * part, part)
-            data[pl.ds(begin, part), :] = piece[...].reshape(part, data.shape[1])
-        gathered = data[...]
-    formed = jnp.dot(gathered, mixer[...], preferred_element_type=F32)
+def unit_of(table, first):
+    unit = (first - FIRST_BLOCK) // 2
+    return table[:, unit * 2 * LANES : (unit + 1) * 2 * LANES]
+
+
+def tile_window(anchors, tile):
+    start = anchors[tile] - tile * TILE_X + LANES
+    lane = lax.broadcasted_iota(jnp.int32, (1, LANES), 1)
+    within = jnp.bitwise_and(start, LANES - 1)
+    return start >= LANES, jnp.bitwise_and(-start, LANES - 1), lane < LANES - within
+
+
+def store_tile(out, tile, c, blocks, window):
+    later, amount, keep = window
+    close = [jnp.where(later, blocks[k + 1], blocks[k]) for k in range(3)]
+    moved = [pltpu.roll(value, amount, 1) for value in close]
+    for half in range(2):
+        value = jnp.where(keep, moved[half], moved[half + 1])
+        out[tile, c, :, half * LANES : (half + 1) * LANES] = value.astype(BF16)
+
+
+def form_beams(data, mixer, left, right):
+    beams = mixer.shape[1] // 2
+    formed = jnp.dot(data, mixer[...], preferred_element_type=F32)
     real = formed[:, :beams].astype(BF16)
     imag = formed[:, beams:].astype(BF16)
     left[:, :beams] = real
     left[:, beams:] = -imag
     right[:, :beams] = imag
     right[:, beams:] = real
+
+
+def gather_pieces(pieces, data, chip):
+    part = data.shape[0] // len(pieces)
+    for step, piece in enumerate(pieces):
+        begin = pl.multiple_of(jnp.bitwise_xor(chip, step) * part, part)
+        data[pl.ds(begin, part), :] = piece[...].reshape(part, data.shape[1])
+    return data[...]
+
+
+def project_tiles(anchors, first_tile, table, left, right, out, common, edge_first, edge_low, edge_high, edge_last,
+                  *, pulses, tiles, width):
+    rows = pulses * width
     last_block = 2 * tiles
 
     def used(first):
@@ -309,8 +333,7 @@
         return min(rows, -(-count * width // 16) * 16)
 
     def product(first, count):
-        unit = (first - FIRST_BLOCK) // 2
-        part = table[:, unit * 2 * LANES : (unit + 1) * 2 * LANES]
+        part = unit_of(table, first)
         return [jnp.dot(side[:count, :], part, preferred_element_type=F32) for side in (left, right)]
 
     for c, value in enumerate(product(0, rows)):
@@ -333,8 +356,6 @@
             for c, value in enumerate(product(first, count)):
                 edge[c, :count, :] = value
 
-    lane = lax.broadcasted_iota(jnp.int32, (1, LANES), 1)
-
     def take(source, c, block, first, half):
         pulse = block - first
         if first > last_block or not 0 <= pulse < pulses:
@@ -349,10 +370,7 @@
         return value
 
     for tile in range(tiles):
-        start = anchors[tile] - tile * TILE_X + LANES
-        far = start >= LANES
-        amount = jnp.bitwise_and(-start, LANES - 1)
-        keep = lane < LANES - jnp.bitwise_and(start, LANES - 1)
+        window = tile_window(anchors, first_tile + tile)
         for c in range(2):
             blocks = []
             for kind in (-1, 0, 1, 2):
@@ -375,21 +393,37 @@
                 else:
                     parts += take(edge_high, c, block - 1, 2 * STEPS - 2, 1)
                 blocks.append(total(parts))
-            close = [jnp.where(far, blocks[k + 1], blocks[k]) for k in range(3)]
-            moved = [pltpu.roll(value, amount, 1) for value in close]
-            for half in range(2):
-                value = jnp.where(keep, moved[half], moved[half + 1])
-                out[tile, c, :, half * LANES : (half + 1) * LANES] = value.astype(BF16)
+            store_tile(out, tile, c, blocks, window)
+
+
+def project_kernel(anchors, mixer, table, *rest, pulses, tiles, width):
+    pieces, (out, data, left, right, *sums) = rest[:-9], rest[-9:]
+    if len(pieces) == 1:
+        gathered = pieces[0][...]
+    else:
+        gathered = gather_pieces(pieces, data, lax.div(lax.axis_index("along"), 2))
+    form_beams(gathered, mixer, left, right)
+    project_tiles(anchors, 0, table, left, right, out, *sums, pulses=pulses, tiles=tiles, width=width)
+
+
+def sum_shapes(rows, tiles, width):
+    span = -(-(2 * tiles + 2) * width // 16) * 16 + 16
+    return [
+        pltpu.VMEM((2, span, 2 * LANES), F32),
+        pltpu.VMEM((2, rows, 2 * LANES), F32),
+        pltpu.VMEM((2, rows, LANES), F32),
+        pltpu.VMEM((2, rows, 2 * LANES), F32),
+        pltpu.VMEM((2, rows, 2 * LANES), F32),
+    ]
 
 
 def project(anchors, pieces, mixer, table, pulses, width):
     rows = pulses * width
     tiles = anchors.shape[0]
     chans, beams = mixer.shape[0], mixer.shape[1] // 2
-    span = -(-(2 * tiles + 2) * width // 16) * 16 + 16
 
     def kernel(*refs):
-        project_kernel(*refs, pulses=pulses, tiles=tiles, width=width, beams=beams)
+        project_kernel(*refs, pulses=pulses, tiles=tiles, width=width)
 
     return pl.pallas_call(
         kernel,
@@ -400,22 +434,148 @@
             pltpu.VMEM((rows, chans), BF16),
             pltpu.VMEM((rows, 2 * beams), BF16),
             pltpu.VMEM((rows, 2 * beams), BF16),
-            pltpu.VMEM((2, span, 2 * LANES), F32),
-            pltpu.VMEM((2, rows, 2 * LANES), F32),
-            pltpu.VMEM((2, rows, LANES), F32),
-            pltpu.VMEM((2, rows, 2 * LANES), F32),
-            pltpu.VMEM((2, rows, 2 * LANES), F32),
+            *sum_shapes(rows, tiles, width),
         ],
         compiler_params=pltpu.CompilerParams(vmem_limit_bytes=24 << 20),
         name="project",
     )(anchors, near(mixer), near(table), *[near(piece) for piece in pieces])
 
 
+def upper_kernel(anchors, mixer, table, *rest, pulses, tiles, width):
+    pieces, (left, right, *sent, data, sums, whole) = rest[: tiles // 2], rest[tiles // 2 :]
+    me = lax.axis_index("along")
+    core = lax.rem(me, 2)
+    group = len(pieces)
+    chip = lax.rem(lax.div(me, 2), group)
+    form_beams(gather_pieces(pieces, data, chip), mixer, left, right)
+    first_block = 2 * tiles - 2
+    last_block = 4 * tiles
+
+    @pl.when(me < tiles)
+    def _():
+        sums[...] = jnp.zeros(sums.shape, F32)
+        for first in range(0, last_block + 1, 2):
+            low = max(0, first_block - first)
+            high = min(pulses - 1, last_block - first)
+            rows = slice(low * width, (high + 1) * width)
+            at = slice((low + first - first_block) * width, (high + 1 + first - first_block) * width)
+            part = unit_of(table, first)
+            for c, side in enumerate((left, right)):
+                sums[c, at, :] = sums[c, at, :] + jnp.dot(side[rows, :], part, preferred_element_type=F32)
+        for tile in range(tiles):
+            window = tile_window(anchors, tiles + tile)
+            for c in range(2):
+                blocks = []
+                for kind in (-1, 0, 1, 2):
+                    row = (2 * (tiles + tile) + kind - first_block) * width
+                    blocks.append(sums[c, row : row + width, :LANES] + sums[c, row - width : row, LANES:])
+                store_tile(whole, tile, c, blocks, window)
+        deal(whole, sent, chip, core)
+
+
+def deal(whole, sent, chip, core):
+    for place, out in enumerate(sent):
+        tile = 2 * jnp.bitwise_xor(chip, place // 2) + jnp.bitwise_xor(core, place % 2)
+        out[...] = whole[tile]
+
+
+def upper_part(anchors, pieces, mixer, table, pulses, width):
+    rows = pulses * width
+    tiles = anchors.shape[0] // 2
+    chans, beams = mixer.shape[0], mixer.shape[1] // 2
+
+    def kernel(*refs):
+        upper_kernel(*refs, pulses=pulses, tiles=tiles, width=width)
+
+    side = pltpu.VMEM((rows, 2 * beams), BF16)
+    left, right, *sent = pl.pallas_call(
+        kernel,
+        out_shape=[side, side] + [pltpu.VMEM((2, width, TILE_X), BF16)] * tiles,
+        in_specs=[pl.BlockSpec(memory_space=pltpu.SMEM)] + [VMEM] * (2 + len(pieces)),
+        out_specs=[VMEM] * (2 + tiles),
+        scratch_shapes=[
+            pltpu.VMEM((rows, chans), BF16),
+            pltpu.VMEM((2, (2 * tiles + 3) * width, 2 * LANES), F32),
+            pltpu.VMEM((tiles, 2, width, TILE_X), BF16),
+        ],
+        compiler_params=pltpu.CompilerParams(vmem_limit_bytes=16 << 20),
+        name="upper_part",
+    )(anchors, near(mixer), near(table), *[near(piece) for piece in pieces])
+    return left, right, sent
+
+
+def own_kernel(anchors, left, right, table, *rest, pulses, tiles, width, group):
+    sent, (whole, *sums) = rest[:-6], rest[-6:]
+    me = lax.axis_index("along")
+    first_tile = lax.div(me, tiles) * tiles
+    project_tiles(anchors, first_tile, table, left, right, whole, *sums, pulses=pulses, tiles=tiles, width=width)
+    deal(whole, sent, lax.rem(lax.div(me, 2), group), lax.rem(me, 2))
+
+
+def own_part(anchors, left, right, table, pulses, width, group):
+    rows = pulses * width
+    tiles = anchors.shape[0] // 2
+
+    def kernel(*refs):
+        own_kernel(*refs, pulses=pulses, tiles=tiles, width=width, group=group)
+
+    return pl.pallas_call(
+        kernel,
+        out_shape=[pltpu.VMEM((2, width, TILE_X), BF16)] * tiles,
+        in_specs=[pl.BlockSpec(memory_space=pltpu.SMEM)] + [VMEM] * 3,
+        out_specs=[VMEM] * tiles,
+        scratch_shapes=[pltpu.VMEM((tiles, 2, width, TILE_X), BF16), *sum_shapes(rows, tiles, width)],
+        compiler_params=pltpu.CompilerParams(vmem_limit_bytes=16 << 20),
+        name="own_part",
+    )(anchors, near(left), near(right), near(table))
+
+
+def same_matrix(size):
+    same = lax.broadcasted_iota(jnp.int32, (size, size), 0) == lax.broadcasted_iota(jnp.int32, (size, size), 1)
+    return same.astype(F32).astype(BF16)
+
+
+def join_kernel(*refs, group):
+    count = 2 * group
+    own, lower, (out, scratch) = refs[:count], refs[count : 2 * count], refs[2 * count :]
+    _, width, pixels = own[0].shape
+    me = lax.axis_index("along")
+    core = lax.rem(me, 2)
+    chip = lax.rem(lax.div(me, 2), group)
+    same = same_matrix(pixels)
+    for place in range(count):
+        part = jnp.bitwise_xor(core, place % 2) * group + jnp.bitwise_xor(chip, place // 2)
+        begin = pl.multiple_of(part * width, width)
+        for c in range(2):
+            value = own[place][c].astype(F32) + lower[place][c].astype(F32)
+            scratch[c, pl.ds(begin, width), :] = value.astype(BF16)
+    for c in range(2):
+        turned = lax.dot_general(same, scratch[c], (((1,), (1,)), ((), ())), preferred_element_type=F32)
+        out[c] = turned.astype(BF16)
+
+
+def join(own, lower, group):
+    _, width, pixels = own[0].shape
+    bins = 2 * group * width
+
+    def kernel(*refs):
+        join_kernel(*refs, group=group)
+
+    return pl.pallas_call(
+        kernel,
+        out_shape=jax.ShapeDtypeStruct((2, pixels, bins), BF16),
+        in_specs=[VMEM] * (4 * group),
+        out_specs=VMEM,
+        scratch_shapes=[pltpu.VMEM((2, bins, pixels), BF16)],
+        compiler_params=pltpu.CompilerParams(vmem_limit_bytes=16 << 20),
+        name="join",
+    )(*[near(value) for value in (*own, *lower)])
+
+
 def turn_kernel(data, out):
     count, _, _, pixels = data.shape
     order = [chip * 2 + core for core in range(2) for chip in range(count // 2)]
-    same = lax.broadcasted_iota(jnp.int32, (pixels, pixels), 0) == lax.broadcasted_iota(jnp.int32, (pixels, pixels), 1)
-    same = same.astype(F32).astype(BF16)
+    same = same_matrix(pixels)
     for c in range(2):
         value = jnp.concatenate([data[source, c] for source in order], 0)
         out[c] = lax.dot_general(same, value, (((1,), (1,)), ((), ())), preferred_element_type=F32).astype(BF16)
@@ -443,24 +603,44 @@
     return order
 
 
+def far_last(chips):
+    return far_first(chips)
+
+
+def in_halves(devices, bins):
+    chips = devices // 2
+    return 8 <= devices <= STEPS and devices & (devices - 1) == 0 and bins // chips % 16 == 0
+
+
 def local(echoes, integer_cell_displacement, fractional_level_label, steering, tile_anchor):
     devices = lax.axis_size("along")
     chips = devices // 2
     pulses, bins = echoes.shape[1], echoes.shape[4]
-    width = bins // devices
-
-    def from_pair(value, step):
-        return lax.ppermute(value, "along", [(i, i ^ step) for i in range(devices)])
+    halves = in_halves(devices, bins)
+    group = chips // 2 if halves else chips
+    width = bins // (2 * group)
+
+    def exchange(value, step, up=False):
+        sources = range(devices // 2 if up else devices)
+        return lax.ppermute(value, "along", [(i, i ^ step) for i in sources])
 
     other_cells, other_levels, other = [
-        from_pair(value, 1) for value in (integer_cell_displacement, fractional_level_label, echoes)
+        exchange(value, 1) for value in (integer_cell_displacement, fractional_level_label, echoes)
     ]
     own, mixer = filter_first(integer_cell_displacement, fractional_level_label, echoes, steering)
-    sent = filter_second(other_cells, other_levels, other, own, chips)
+    sent = filter_second(other_cells, other_levels, other, own, group)
     table = make_table(steering.shape[2], pulses)
-    pieces = [sent[0]] + [None] * (chips - 1)
-    for k in far_first(chips):
-        pieces[k] = from_pair(sent[k], 2 * k)
+    pieces = [sent[0]] + [None] * (group - 1)
+    for k in far_first(group):
+        pieces[k] = exchange(sent[k], 2 * k)
+    if halves:
+        left, right, upper = upper_part(tile_anchor, pieces, mixer, table, chips * pulses, width)
+        lower = [exchange(upper[k], devices // 2 + k, up=True) for k in range(chips)]
+        parts = own_part(tile_anchor, left, right, table, chips * pulses, width, group)
+        owned = [parts[0]] + [None] * (chips - 1)
+        for k in (*far_last(chips),):
+            owned[k] = exchange(parts[k], k)
+        return join(owned, lower, group)
     if width % 16:
         chip = lax.axis_index("along") // 2
         order = jnp.bitwise_xor(jnp.arange(chips), chip)

time: 43 us -> 44.6 us (1.037)
  blocking collectives: 14.6 us -> 0 us
  starting transfers between devices: 13.1 us -> 25.1 us
  Pallas kernels: 11.1 us -> 13.7 us
  waiting for transfers between devices: 4.06 us -> 5.24 us
    all_to_all x1 -> x0, blocking collectives: 14.6 us -> none  [local(): return turn(lax.all_to_all(finished, 'along', 0, 0, tiled=True))]
    ppermute x10 -> x21, starting transfers between devices: 13.1 us -> 25.1 us  [exchange(): return lax.ppermute(value, 'along', [(i, i ^ step) for i in sources])]
    pallas_call x2 -> x3, Pallas kernels: 4.91 us -> 7.54 us  [the longest x1 3.94 us: upper_part(): pl.pallas_call(kernel, out_shape=[side, side] + [pltpu.VMEM((2, width, TI...]
    ppermute x10 -> x21, waiting for transfers between devices: 4.06 us -> 5.24 us  [exchange(): return lax.ppermute(value, 'along', [(i, i ^ step) for i in sources])]
  transfers between devices with their start and end apart: 10 -> 21, of which waited for: 2 -> 4; matrix products, arithmetic and copies ran while one was open for 0% -> 0% of each run, Pallas kernels for 12% -> 12%
where the time goes in v1:
time: 44.6 us; the launch traced here: 44.3 us
  starting transfers between devices  25.1 us (56%)
  Pallas kernels  13.7 us (31%)
  waiting for transfers between devices  5.24 us (12%)
    ppermute x21, starting transfers between devices, exchange(): return lax.ppermute(value, 'along', [(i, i ^ step) for i in sources])  25.1 us
    ppermute x21, waiting for transfers between devices, exchange(): return lax.ppermute(value, 'along', [(i, i ^ step) for i in sources])  5.24 us
    pallas_call x1, Pallas kernels, upper_part(): pl.pallas_call(kernel, out_shape=[side, side] + [pltpu.VMEM((2, width, TI...  3.94 us
    pallas_call x1, Pallas kernels, make_table(): pl.pallas_call(kernel, out_shape=pltpu.VMEM((2 * beams, 2 * UNITS * LANES...  2.97 us
    pallas_call x1, Pallas kernels, own_part(): pl.pallas_call(kernel, out_shape=[pltpu.VMEM((2, width, TILE_X), BF16)] *...  2.58 us
    pallas_call x1, Pallas kernels, filter_first(): pl.pallas_call(first_kernel, out_shape=(pltpu.VMEM((pulses, bins // 2, 2...  2.16 us
    pallas_call x1, Pallas kernels, filter_second(): pl.pallas_call(kernel, out_shape=[pltpu.VMEM(shape, BF16)] * count, in_sp...  1.04 us
    pallas_call x1, Pallas kernels, join(): pl.pallas_call(kernel, out_shape=jax.ShapeDtypeStruct((2, pixels, bins),...  1.02 us
  transfers between devices with their start and end apart: 21, of which 4 were waited for; matrix products, arithmetic and copies ran while one was open for 0% of the time, Pallas kernels for 12%

profile of v1, /device:TPU:0, one launch (start us, length us, event | category | flops | bytes accessed | tf_op | source)
XLA Modules:
  0.0 44.3 jit_solution(421788384918786702)
XLA Ops:
  0.0 0.5 %collective-permute-start.2 = (bf16[2,2,16,16,256]{4,3,2,1,0:T(8,128)(2,1)}, bf16[2,2,16,16,256]{4,3,2,1,0:T(8,128)(2,1)S(1)}, u32[]{:S(2)}, u32[]{:S(2)}) collective-permute-start(bf16[2,2,16,16,256]{4,3,2,1,0:T(8,128)(2,1)} %echo.1), channel_id=1, source_target_pairs={{0,1},{1,0},{2,3},{3,2},{4,5},{5,4},{6,7},{7,6},{8,9},{9,8},{10,11... | collective-permute-start | bytes 1572872 | tf_op jit(solution)/shard_map/ppermute | solution.py:625
  0.5 0.0 collective-permute-start
  0.5 0.5 %collective-permute-start.1 = (s32[2,16]{1,0:T(2,128)}, s32[2,16]{1,0:T(2,128)S(1)}, u32[]{:S(2)}, u32[]{:S(2)}) collective-permute-start(s32[2,16]{1,0:T(2,128)} %levels.1), channel_id=1, source_target_pairs={{0,1},{1,0},{2,3},{3,2},{4,5},{5,4},{6,7},{7,6},{8,9},{9,8},{10,11... | collective-permute-start | bytes 392 | tf_op jit(solution)/shard_map/ppermute | solution.py:625
  1.0 2.2 %filter_first.1 = (bf16[2,128,512]{2,1,0:T(8,128)(2,1)S(1)}, bf16[512,512]{1,0:T(8,128)(2,1)S(1)}) custom-call(s32[2,16]{1,0:T(2,128)} %cells.1, s32[2,16]{1,0:T(2,128)} %levels.1, bf16[2,2,16,16,256]{4,3,2,1,0:T(8,128)(2,1)} %echo.1, bf16[2,256,256]{2,1,0:T(8,128)(2,1)} %steering.1), custom_call_target="tpu_custom_call" | custom-call | flops 100000000 | tf_op jit(solution)/shard_map/filter_first/pallas_call | solution.py:191
  3.2 0.0 collective-permute-done.refs_0_
  3.2 0.0 collective-permute-done.1.refs_1_
  3.2 0.0 collective-permute-done.2.refs_2_
  3.2 1.0 %filter_second.1 = (bf16[4,32,512]{2,1,0:T(8,128)(2,1)S(1)}, bf16[4,32,512]{2,1,0:T(8,128)(2,1)S(1)}, bf16[4,32,512]{2,1,0:T(8,128)(2,1)S(1)}, bf16[4,32,512]{2,1,0:T(8,128)(2,1)S(1)}) custom-call(s32[2,16]{1,0:T(2,128)S(1)} %collective-permute-done.refs_0_, s32[2,16]{1,0:T(2,128)S(1)} %collective-permute-done.1.refs_1_, ...), custom_call_target="tpu_custom_call" | custom-call | tf_op jit(solution)/shard_map/filter_second/pallas_call | solution.py:221
  4.2 2.6 %collective-permute-start.3 = (bf16[4,32,512]{2,1,0:T(8,128)(2,1)S(1)}, bf16[4,32,512]{2,1,0:T(8,128)(2,1)S(1)}, u32[]{:S(2)}, u32[]{:S(2)}) collective-permute-start(bf16[4,32,512]{2,1,0:T(8,128)(2,1)S(1)} %get-tuple-element.32), channel_id=1, source_target_pairs={{0,2},{1,3},{2,0},{3,1},{4,6},{5,7},{6,4},{7,5},{8,10},{9,11},{10,... | collective-permute-start | bytes 393224 | tf_op jit(solution)/shard_map/ppermute | solution.py:625
  6.8 1.6 %collective-permute-start.4 = (bf16[4,32,512]{2,1,0:T(8,128)(2,1)S(1)}, bf16[4,32,512]{2,1,0:T(8,128)(2,1)S(1)}, u32[]{:S(2)}, u32[]{:S(2)}) collective-permute-start(bf16[4,32,512]{2,1,0:T(8,128)(2,1)S(1)} %get-tuple-element.33), channel_id=1, source_target_pairs={{0,4},{1,5},{2,6},{3,7},{4,0},{5,1},{6,2},{7,3},{8,12},{9,13},{10,... | collective-permute-start | bytes 393224 | tf_op jit(solution)/shard_map/ppermute | solution.py:625
  8.4 0.0 collective-permute-start.5
  8.4 3.0 %table.1.refs_2_.refs_3_ = bf16[512,4608]{1,0:T(8,128)(2,1)S(1)} custom-call(), custom_call_target="tpu_custom_call" | custom-call | flops 4718592000 | tf_op jit(solution)/shard_map/table/pallas_call | solution.py:275
  11.4 0.0 collective-permute-done.3.refs_4_
  11.4 1.8 %collective-permute-done.4.refs_5_ = bf16[4,32,512]{2,1,0:T(8,128)(2,1)S(1)} collective-permute-done((bf16[4,32,512]{2,1,0:T(8,128)(2,1)S(1)}, bf16[4,32,512]{2,1,0:T(8,128)(2,1)S(1)}, u32[]{:S(2)}, u32[]{:S(2)}) %collective-permute-start.4) | collective-permute-done | bytes 131104 | tf_op jit(solution)/shard_map/ppermute | solution.py:625
  13.2 1.9 %collective-permute-done.5.refs_6_ = bf16[4,32,512]{2,1,0:T(8,128)(2,1)S(1)} collective-permute-done((bf16[4,32,512]{2,1,0:T(8,128)(2,1)S(1)}, bf16[4,32,512]{2,1,0:T(8,128)(2,1)S(1)}, u32[]{:S(2)}, u32[]{:S(2)}) %collective-permute-start.5) | collective-permute-done | bytes 131104 | tf_op jit(solution)/shard_map/ppermute | solution.py:625
  15.1 3.9 %upper_part.1 = (bf16[512,512]{1,0:T(8,128)(2,1)S(1)}, bf16[512,512]{1,0:T(8,128)(2,1)S(1)}, bf16[2,32,256]{2,1,0:T(8,128)(2,1)S(1)}, bf16[2,32,256]{2,1,0:T(8,1...) custom-call(s32[16]{0:T(128)S(1)} %copy-done, ...), custom_call_target="tpu_custom_call" | custom-call | tf_op jit(solution)/shard_map/upper_part/pallas_call | solution.py:491
  19.0 2.6 %own_part.1 = (bf16[2,32,256]{2,1,0:T(8,128)(2,1)S(1)}, bf16[2,32,256]{2,1,0:T(8,128)(2,1)S(1)}, bf16[2,32,256]{2,1,0:T(8,128)(2,1)S(1)}, bf16[2,32,256]{2,1,0:T...) custom-call(s32[16]{0:T(128)S(1)} %copy-done, ...), custom_call_target="tpu_custom_call" | custom-call | tf_op jit(solution)/shard_map/own_part/pallas_call | solution.py:522
  21.6 0.1 collective-permute-start.6
  21.7 1.7 %collective-permute-start.7 = (bf16[2,32,256]{2,1,0:T(8,128)(2,1)S(1)}, bf16[2,32,256]{2,1,0:T(8,128)(2,1)S(1)}, u32[]{:S(2)}, u32[]{:S(2)}) collective-permute-start(bf16[2,32,256]{2,1,0:T(8,128)(2,1)S(1)} %get-tuple-element.39), channel_id=1, source_target_pairs={{0,2},{1,3},{2,0},{3,1},{4,6},{5,7},{6,4},{7,5},{8,10},{9,11},{10,... | collective-permute-start | bytes 98312 | tf_op jit(solution)/shard_map/ppermute | solution.py:625
  23.4 0.1 collective-permute-start.8
  23.5 1.7 %collective-permute-start.9 = (bf16[2,32,256]{2,1,0:T(8,128)(2,1)S(1)}, bf16[2,32,256]{2,1,0:T(8,128)(2,1)S(1)}, u32[]{:S(2)}, u32[]{:S(2)}) collective-permute-start(bf16[2,32,256]{2,1,0:T(8,128)(2,1)S(1)} %get-tuple-element.41), channel_id=1, source_target_pairs={{0,4},{1,5},{2,6},{3,7},{4,0},{5,1},{6,2},{7,3},{8,12},{9,13},{10,... | collective-permute-start | bytes 98312 | tf_op jit(solution)/shard_map/ppermute | solution.py:625
  25.2 0.0 collective-permute-start.10
  25.2 0.0 collective-permute-done.6.refs_1_
  25.2 2.7 %collective-permute-start.11 = (bf16[2,32,256]{2,1,0:T(8,128)(2,1)S(1)}, bf16[2,32,256]{2,1,0:T(8,128)(2,1)S(1)}, u32[]{:S(2)}, u32[]{:S(2)}) collective-permute-start(bf16[2,32,256]{2,1,0:T(8,128)(2,1)S(1)} %get-tuple-element.43), channel_id=1, source_target_pairs={{0,6},{1,7},{2,4},{3,5},{4,2},{5,3},{6,0},{7,1},{8,14},{9,15},{10,... | collective-permute-start | bytes 98312 | tf_op jit(solution)/shard_map/ppermute | solution.py:625
  27.9 0.0 collective-permute-done.7.refs_2_
  27.9 0.1 collective-permute-start.12
  28.0 0.0 collective-permute-done.8.refs_3_
  28.0 1.6 %collective-permute-start.13 = (bf16[2,32,256]{2,1,0:T(8,128)(2,1)S(1)}, bf16[2,32,256]{2,1,0:T(8,128)(2,1)S(1)}, u32[]{:S(2)}, u32[]{:S(2)}) collective-permute-start(bf16[2,32,256]{2,1,0:T(8,128)(2,1)S(1)} %get-tuple-element.45), channel_id=1, source_target_pairs={{0,8},{1,9},{2,10},{3,11},{4,12},{5,13},{6,14},{7,15},{16,24},{17,... | collective-permute-start | bytes 98312 | tf_op jit(solution)/shard_map/ppermute | solution.py:625
  29.6 0.0 collective-permute-done.9.refs_4_
  29.6 1.6 %collective-permute-start.14 = (bf16[2,32,256]{2,1,0:T(8,128)(2,1)S(1)}, bf16[2,32,256]{2,1,0:T(8,128)(2,1)S(1)}, u32[]{:S(2)}, u32[]{:S(2)}) collective-permute-start(bf16[2,32,256]{2,1,0:T(8,128)(2,1)S(1)} %get-tuple-element.46), channel_id=1, source_target_pairs={{0,9},{1,8},{2,11},{3,10},{4,13},{5,12},{6,15},{7,14},{16,25},{17,... | collective-permute-start | bytes 98312 | tf_op jit(solution)/shard_map/ppermute | solution.py:625
  31.2 0.0 collective-permute-done.10.refs_5_
  31.2 2.0 %collective-permute-start.15 = (bf16[2,32,256]{2,1,0:T(8,128)(2,1)S(1)}, bf16[2,32,256]{2,1,0:T(8,128)(2,1)S(1)}, u32[]{:S(2)}, u32[]{:S(2)}) collective-permute-start(bf16[2,32,256]{2,1,0:T(8,128)(2,1)S(1)} %get-tuple-element.47), channel_id=1, source_target_pairs={{0,10},{1,11},{2,8},{3,9},{4,14},{5,15},{6,12},{7,13},{16,26},{17,... | collective-permute-start | bytes 98312 | tf_op jit(solution)/shard_map/ppermute | solution.py:625
  33.2 0.0 collective-permute-done.11.refs_6_
  33.2 1.3 %collective-permute-start.16 = (bf16[2,32,256]{2,1,0:T(8,128)(2,1)S(1)}, bf16[2,32,256]{2,1,0:T(8,128)(2,1)S(1)}, u32[]{:S(2)}, u32[]{:S(2)}) collective-permute-start(bf16[2,32,256]{2,1,0:T(8,128)(2,1)S(1)} %get-tuple-element.48), channel_id=1, source_target_pairs={{0,11},{1,10},{2,9},{3,8},{4,15},{5,14},{6,13},{7,12},{16,27},{17,... | collective-permute-start | bytes 98312 | tf_op jit(solution)/shard_map/ppermute | solution.py:625
  34.5 0.0 collective-permute-done.12.refs_7_
  34.5 1.3 %collective-permute-start.17 = (bf16[2,32,256]{2,1,0:T(8,128)(2,1)S(1)}, bf16[2,32,256]{2,1,0:T(8,128)(2,1)S(1)}, u32[]{:S(2)}, u32[]{:S(2)}) collective-permute-start(bf16[2,32,256]{2,1,0:T(8,128)(2,1)S(1)} %get-tuple-element.49), channel_id=1, source_target_pairs={{0,12},{1,13},{2,14},{3,15},{4,8},{5,9},{6,10},{7,11},{16,28},{17,... | collective-permute-start | bytes 98312 | tf_op jit(solution)/shard_map/ppermute | solution.py:625
  35.9 0.0 collective-permute-done.13.refs_8_
  35.9 1.3 %collective-permute-start.18 = (bf16[2,32,256]{2,1,0:T(8,128)(2,1)S(1)}, bf16[2,32,256]{2,1,0:T(8,128)(2,1)S(1)}, u32[]{:S(2)}, u32[]{:S(2)}) collective-permute-start(bf16[2,32,256]{2,1,0:T(8,128)(2,1)S(1)} %get-tuple-element.50), channel_id=1, source_target_pairs={{0,13},{1,12},{2,15},{3,14},{4,9},{5,8},{6,11},{7,10},{16,29},{17,... | collective-permute-start | bytes 98312 | tf_op jit(solution)/shard_map/ppermute | solution.py:625
  37.2 0.0 collective-permute-done.14.refs_9_
  37.2 3.1 %collective-permute-start.19 = (bf16[2,32,256]{2,1,0:T(8,128)(2,1)S(1)}, bf16[2,32,256]{2,1,0:T(8,128)(2,1)S(1)}, u32[]{:S(2)}, u32[]{:S(2)}) collective-permute-start(bf16[2,32,256]{2,1,0:T(8,128)(2,1)S(1)} %get-tuple-element.51), channel_id=1, source_target_pairs={{0,14},{1,15},{2,12},{3,13},{4,10},{5,11},{6,8},{7,9},{16,30},{17,... | collective-permute-start | bytes 98312 | tf_op jit(solution)/shard_map/ppermute | solution.py:625
  40.4 0.0 collective-permute-done.15.refs_10_
  40.4 1.3 %collective-permute-start.20 = (bf16[2,32,256]{2,1,0:T(8,128)(2,1)S(1)}, bf16[2,32,256]{2,1,0:T(8,128)(2,1)S(1)}, u32[]{:S(2)}, u32[]{:S(2)}) collective-permute-start(bf16[2,32,256]{2,1,0:T(8,128)(2,1)S(1)} %get-tuple-element.52), channel_id=1, source_target_pairs={{0,15},{1,14},{2,13},{3,12},{4,11},{5,10},{6,9},{7,8},{16,31},{17,... | collective-permute-start | bytes 98312 | tf_op jit(solution)/shard_map/ppermute | solution.py:625
  41.7 0.0 collective-permute-done.16.refs_11_
  41.7 0.0 collective-permute-done.17.refs_12_
  41.7 0.0 collective-permute-done.18.refs_13_
  41.7 0.2 collective-permute-done.19.refs_14_
  41.9 1.3 %collective-permute-done.20.refs_15_ = bf16[2,32,256]{2,1,0:T(8,128)(2,1)S(1)} collective-permute-done((bf16[2,32,256]{2,1,0:T(8,128)(2,1)S(1)}, bf16[2,32,256]{2,1,0:T(8,128)(2,1)S(1)}, u32[]{:S(2)}, u32[]{:S(2)}) %collective-permute-start.20) | collective-permute-done | bytes 32800 | tf_op jit(solution)/shard_map/ppermute | solution.py:625
  43.2 1.0 %join.1 = bf16[2,256,256]{2,1,0:T(8,128)(2,1)} custom-call(bf16[2,32,256]{2,1,0:T(8,128)(2,1)S(1)} %get-tuple-element.37.refs_0_, bf16[2,32,256]{2,1,0:T(8,128)(2,1)S(1)} %collective-permute-done.6.refs_1_, bf16[2,32,256]{2,1,0:T(8,128)(2,1)S(1)} %collective-permute-done.7.refs_2_, bf16[2,32,256]{2,1,0:T(8,128)(2,1)S(1)} %collective-permute-done.8.refs_3_, ...), custom_call_target="tpu_custom_call" | custom-call | tf_op jit(solution)/shard_map/join/pallas_call | solution.py:564
  (2 shorter events, 0.0 us)
Async XLA Ops:
  0.0 3.2 %collective-permute-start.2 = (bf16[2,2,16,16,256]{4,3,2,1,0:T(8,128)(2,1)}, bf16[2,2,16,16,256]{4,3,2,1,0:T(8,128)(2,1)S(1)}, u32[]{:S(2)}, u32[]{:S(2)}) collective-permute-start(bf16[2,2,16,16,256]{4,3,2,1,0:T(8,128)(2,1)} %echo.1), channel_id=1, source_target_pairs={{0,1},{1,0},{2,3},{3,2},{4,5},{5,4},{6,7},{7,6},{8,9},{9,8},{10,11... | collective-permute-start | bytes 1572872 | tf_op jit(solution)/shard_map/ppermute | solution.py:625
  0.5 2.7 %collective-permute-start = (s32[2,16]{1,0:T(2,128)}, s32[2,16]{1,0:T(2,128)S(1)}, u32[]{:S(2)}, u32[]{:S(2)}) collective-permute-start(s32[2,16]{1,0:T(2,128)} %cells.1), channel_id=1, source_target_pairs={{0,1},{1,0},{2,3},{3,2},{4,5},{5,4},{6,7},{7,6},{8,9},{9,8},{10,11... | collective-permute-start | bytes 392 | tf_op jit(solution)/shard_map/ppermute | solution.py:625
  0.5 2.7 %collective-permute-start.1 = (s32[2,16]{1,0:T(2,128)}, s32[2,16]{1,0:T(2,128)S(1)}, u32[]{:S(2)}, u32[]{:S(2)}) collective-permute-start(s32[2,16]{1,0:T(2,128)} %levels.1), channel_id=1, source_target_pairs={{0,1},{1,0},{2,3},{3,2},{4,5},{5,4},{6,7},{7,6},{8,9},{9,8},{10,11... | collective-permute-start | bytes 392 | tf_op jit(solution)/shard_map/ppermute | solution.py:625
  4.2 7.1 %collective-permute-start.3 = (bf16[4,32,512]{2,1,0:T(8,128)(2,1)S(1)}, bf16[4,32,512]{2,1,0:T(8,128)(2,1)S(1)}, u32[]{:S(2)}, u32[]{:S(2)}) collective-permute-start(bf16[4,32,512]{2,1,0:T(8,128)(2,1)S(1)} %get-tuple-element.32), channel_id=1, source_target_pairs={{0,2},{1,3},{2,0},{3,1},{4,6},{5,7},{6,4},{7,5},{8,10},{9,11},{10,... | collective-permute-start | bytes 393224 | tf_op jit(solution)/shard_map/ppermute | solution.py:625
  6.8 6.4 %collective-permute-start.4 = (bf16[4,32,512]{2,1,0:T(8,128)(2,1)S(1)}, bf16[4,32,512]{2,1,0:T(8,128)(2,1)S(1)}, u32[]{:S(2)}, u32[]{:S(2)}) collective-permute-start(bf16[4,32,512]{2,1,0:T(8,128)(2,1)S(1)} %get-tuple-element.33), channel_id=1, source_target_pairs={{0,4},{1,5},{2,6},{3,7},{4,0},{5,1},{6,2},{7,3},{8,12},{9,13},{10,... | collective-permute-start | bytes 393224 | tf_op jit(solution)/shard_map/ppermute | solution.py:625
  8.4 6.6 %copy-start = (s32[16]{0:T(128)S(1)}, s32[16]{0:T(128)}, u32[]{:S(2)}) copy-start(s32[16]{0:T(128)} %refs_0_.3) | copy-start | bytes 196
  8.4 6.6 %collective-permute-start.5 = (bf16[4,32,512]{2,1,0:T(8,128)(2,1)S(1)}, bf16[4,32,512]{2,1,0:T(8,128)(2,1)S(1)}, u32[]{:S(2)}, u32[]{:S(2)}) collective-permute-start(bf16[4,32,512]{2,1,0:T(8,128)(2,1)S(1)} %get-tuple-element.34), channel_id=1, source_target_pairs={{0,6},{1,7},{2,4},{3,5},{4,2},{5,3},{6,0},{7,1},{8,14},{9,15},{10,... | collective-permute-start | bytes 393224 | tf_op jit(solution)/shard_map/ppermute | solution.py:625
  21.6 3.7 %collective-permute-start.6 = (bf16[2,32,256]{2,1,0:T(8,128)(2,1)S(1)}, bf16[2,32,256]{2,1,0:T(8,128)(2,1)S(1)}, u32[]{:S(2)}, u32[]{:S(2)}) collective-permute-start(bf16[2,32,256]{2,1,0:T(8,128)(2,1)S(1)} %get-tuple-element.38), channel_id=1, source_target_pairs={{0,1},{1,0},{2,3},{3,2},{4,5},{5,4},{6,7},{7,6},{8,9},{9,8},{10,11... | collective-permute-start | bytes 98312 | tf_op jit(solution)/shard_map/ppermute | solution.py:625
  21.7 6.3 %collective-permute-start.7 = (bf16[2,32,256]{2,1,0:T(8,128)(2,1)S(1)}, bf16[2,32,256]{2,1,0:T(8,128)(2,1)S(1)}, u32[]{:S(2)}, u32[]{:S(2)}) collective-permute-start(bf16[2,32,256]{2,1,0:T(8,128)(2,1)S(1)} %get-tuple-element.39), channel_id=1, source_target_pairs={{0,2},{1,3},{2,0},{3,1},{4,6},{5,7},{6,4},{7,5},{8,10},{9,11},{10,... | collective-permute-start | bytes 98312 | tf_op jit(solution)/shard_map/ppermute | solution.py:625
  23.4 4.6 %collective-permute-start.8 = (bf16[2,32,256]{2,1,0:T(8,128)(2,1)S(1)}, bf16[2,32,256]{2,1,0:T(8,128)(2,1)S(1)}, u32[]{:S(2)}, u32[]{:S(2)}) collective-permute-start(bf16[2,32,256]{2,1,0:T(8,128)(2,1)S(1)} %get-tuple-element.40), channel_id=1, source_target_pairs={{0,3},{1,2},{2,1},{3,0},{4,7},{5,6},{6,5},{7,4},{8,11},{9,10},{10,... | collective-permute-start | bytes 98312 | tf_op jit(solution)/shard_map/ppermute | solution.py:625
  23.5 6.1 %collective-permute-start.9 = (bf16[2,32,256]{2,1,0:T(8,128)(2,1)S(1)}, bf16[2,32,256]{2,1,0:T(8,128)(2,1)S(1)}, u32[]{:S(2)}, u32[]{:S(2)}) collective-permute-start(bf16[2,32,256]{2,1,0:T(8,128)(2,1)S(1)} %get-tuple-element.41), channel_id=1, source_target_pairs={{0,4},{1,5},{2,6},{3,7},{4,0},{5,1},{6,2},{7,3},{8,12},{9,13},{10,... | collective-permute-start | bytes 98312 | tf_op jit(solution)/shard_map/ppermute | solution.py:625
  25.2 6.0 %collective-permute-start.10 = (bf16[2,32,256]{2,1,0:T(8,128)(2,1)S(1)}, bf16[2,32,256]{2,1,0:T(8,128)(2,1)S(1)}, u32[]{:S(2)}, u32[]{:S(2)}) collective-permute-start(bf16[2,32,256]{2,1,0:T(8,128)(2,1)S(1)} %get-tuple-element.42), channel_id=1, source_target_pairs={{0,5},{1,4},{2,7},{3,6},{4,1},{5,0},{6,3},{7,2},{8,13},{9,12},{10,... | collective-permute-start | bytes 98312 | tf_op jit(solution)/shard_map/ppermute | solution.py:625
  25.2 8.0 %collective-permute-start.11 = (bf16[2,32,256]{2,1,0:T(8,128)(2,1)S(1)}, bf16[2,32,256]{2,1,0:T(8,128)(2,1)S(1)}, u32[]{:S(2)}, u32[]{:S(2)}) collective-permute-start(bf16[2,32,256]{2,1,0:T(8,128)(2,1)S(1)} %get-tuple-element.43), channel_id=1, source_target_pairs={{0,6},{1,7},{2,4},{3,5},{4,2},{5,3},{6,0},{7,1},{8,14},{9,15},{10,... | collective-permute-start | bytes 98312 | tf_op jit(solution)/shard_map/ppermute | solution.py:625
  27.9 6.6 %collective-permute-start.12 = (bf16[2,32,256]{2,1,0:T(8,128)(2,1)S(1)}, bf16[2,32,256]{2,1,0:T(8,128)(2,1)S(1)}, u32[]{:S(2)}, u32[]{:S(2)}) collective-permute-start(bf16[2,32,256]{2,1,0:T(8,128)(2,1)S(1)} %get-tuple-element.44), channel_id=1, source_target_pairs={{0,7},{1,6},{2,5},{3,4},{4,3},{5,2},{6,1},{7,0},{8,15},{9,14},{10,... | collective-permute-start | bytes 98312 | tf_op jit(solution)/shard_map/ppermute | solution.py:625
  28.0 7.8 %collective-permute-start.13 = (bf16[2,32,256]{2,1,0:T(8,128)(2,1)S(1)}, bf16[2,32,256]{2,1,0:T(8,128)(2,1)S(1)}, u32[]{:S(2)}, u32[]{:S(2)}) collective-permute-start(bf16[2,32,256]{2,1,0:T(8,128)(2,1)S(1)} %get-tuple-element.45), channel_id=1, source_target_pairs={{0,8},{1,9},{2,10},{3,11},{4,12},{5,13},{6,14},{7,15},{16,24},{17,... | collective-permute-start | bytes 98312 | tf_op jit(solution)/shard_map/ppermute | solution.py:625
  29.6 7.6 %collective-permute-start.14 = (bf16[2,32,256]{2,1,0:T(8,128)(2,1)S(1)}, bf16[2,32,256]{2,1,0:T(8,128)(2,1)S(1)}, u32[]{:S(2)}, u32[]{:S(2)}) collective-permute-start(bf16[2,32,256]{2,1,0:T(8,128)(2,1)S(1)} %get-tuple-element.46), channel_id=1, source_target_pairs={{0,9},{1,8},{2,11},{3,10},{4,13},{5,12},{6,15},{7,14},{16,25},{17,... | collective-permute-start | bytes 98312 | tf_op jit(solution)/shard_map/ppermute | solution.py:625
  31.2 9.2 %collective-permute-start.15 = (bf16[2,32,256]{2,1,0:T(8,128)(2,1)S(1)}, bf16[2,32,256]{2,1,0:T(8,128)(2,1)S(1)}, u32[]{:S(2)}, u32[]{:S(2)}) collective-permute-start(bf16[2,32,256]{2,1,0:T(8,128)(2,1)S(1)} %get-tuple-element.47), channel_id=1, source_target_pairs={{0,10},{1,11},{2,8},{3,9},{4,14},{5,15},{6,12},{7,13},{16,26},{17,... | collective-permute-start | bytes 98312 | tf_op jit(solution)/shard_map/ppermute | solution.py:625
  33.2 8.5 %collective-permute-start.16 = (bf16[2,32,256]{2,1,0:T(8,128)(2,1)S(1)}, bf16[2,32,256]{2,1,0:T(8,128)(2,1)S(1)}, u32[]{:S(2)}, u32[]{:S(2)}) collective-permute-start(bf16[2,32,256]{2,1,0:T(8,128)(2,1)S(1)} %get-tuple-element.48), channel_id=1, source_target_pairs={{0,11},{1,10},{2,9},{3,8},{4,15},{5,14},{6,13},{7,12},{16,27},{17,... | collective-permute-start | bytes 98312 | tf_op jit(solution)/shard_map/ppermute | solution.py:625
  34.5 7.2 %collective-permute-start.17 = (bf16[2,32,256]{2,1,0:T(8,128)(2,1)S(1)}, bf16[2,32,256]{2,1,0:T(8,128)(2,1)S(1)}, u32[]{:S(2)}, u32[]{:S(2)}) collective-permute-start(bf16[2,32,256]{2,1,0:T(8,128)(2,1)S(1)} %get-tuple-element.49), channel_id=1, source_target_pairs={{0,12},{1,13},{2,14},{3,15},{4,8},{5,9},{6,10},{7,11},{16,28},{17,... | collective-permute-start | bytes 98312 | tf_op jit(solution)/shard_map/ppermute | solution.py:625
  35.9 5.8 %collective-permute-start.18 = (bf16[2,32,256]{2,1,0:T(8,128)(2,1)S(1)}, bf16[2,32,256]{2,1,0:T(8,128)(2,1)S(1)}, u32[]{:S(2)}, u32[]{:S(2)}) collective-permute-start(bf16[2,32,256]{2,1,0:T(8,128)(2,1)S(1)} %get-tuple-element.50), channel_id=1, source_target_pairs={{0,13},{1,12},{2,15},{3,14},{4,9},{5,8},{6,11},{7,10},{16,29},{17,... | collective-permute-start | bytes 98312 | tf_op jit(solution)/shard_map/ppermute | solution.py:625
  37.2 4.7 %collective-permute-start.19 = (bf16[2,32,256]{2,1,0:T(8,128)(2,1)S(1)}, bf16[2,32,256]{2,1,0:T(8,128)(2,1)S(1)}, u32[]{:S(2)}, u32[]{:S(2)}) collective-permute-start(bf16[2,32,256]{2,1,0:T(8,128)(2,1)S(1)} %get-tuple-element.51), channel_id=1, source_target_pairs={{0,14},{1,15},{2,12},{3,13},{4,10},{5,11},{6,8},{7,9},{16,30},{17,... | collective-permute-start | bytes 98312 | tf_op jit(solution)/shard_map/ppermute | solution.py:625
  40.4 2.9 %collective-permute-start.20 = (bf16[2,32,256]{2,1,0:T(8,128)(2,1)S(1)}, bf16[2,32,256]{2,1,0:T(8,128)(2,1)S(1)}, u32[]{:S(2)}, u32[]{:S(2)}) collective-permute-start(bf16[2,32,256]{2,1,0:T(8,128)(2,1)S(1)} %get-tuple-element.52), channel_id=1, source_target_pairs={{0,15},{1,14},{2,13},{3,12},{4,11},{5,10},{6,9},{7,8},{16,31},{17,... | collective-permute-start | bytes 98312 | tf_op jit(solution)/shard_map/ppermute | solution.py:625
